TPU v7x, 512 devices: a whole 4x4x16 slice. The times are simulated.
512 devices in a mesh: grp: 8 (over y_lo, x), shard: 64 (over z, y_hi, core).
Axes of the slice: x: 4, y: 4 (y_hi: 2, y_lo: 2; y = y_hi * 2 + y_lo), z: 16, core: 2. Of those that a mesh axis runs over, the one named last changes fastest.
Arguments:
- window: bfloat16 [128, 4096], P('grp'), may hold values from -6 to 6
- weight: bfloat16 [11008, 4096], P('shard'), may hold values from -0.09375 to 0.09375
- factor_a: bfloat16 [1024, 4, 4096], P(('grp', 'shard')), may hold values from -6 to 6
- factor_b: bfloat16 [1024, 4, 11008], P(('grp', 'shard')), may hold values from -6 to 6
- fitness: float32 [1024], P(('grp', 'shard')), may hold values from -4 to 4
Outputs:
- perturbed: bfloat16 [11008, 16384], P('shard', 'grp')
- update: float32 [11008, 4096], P('shard', 'grp')
All inputs are finite; a program needn't handle non-finite values.
Results may differ from a plain program's by a relative error of at most 0.0029.
Values may be sent and summed in bfloat16 or wider, within the bound.
A program may use at most 64 MiB of HBM per device.

v0:
```python
import math

import jax
import jax.numpy as jnp
from jax import lax
from jax.sharding import Mesh
from jax.sharding import PartitionSpec as P

SHARD = ("shard_0", "shard_1", "shard_2")
GRP_SHARD = ("grp", "shard_0", "shard_1", "shard_2")


def side_by_side(arrays, axis, dim, along):
    columns = [a.reshape(*a.shape[:along], -1) for a in arrays]
    both = jnp.concatenate(columns, axis=along)
    filled, at, done = (lax.all_gather(both, axis, axis=dim, tiled=True), 0, [])
    for a, column in zip(arrays, columns):
        share = filled[..., at : at + column.shape[along]]
        done.append(share.reshape(*share.shape[:along], *a.shape[along:]))
        at += column.shape[along]
    return tuple(done)


def from_everyone(value, axis):
    peers = lax.axis_size(axis)
    return lax.all_to_all(
        jnp.broadcast_to(value[None], (peers, *value.shape)), axis, 0, 0, tiled=True
    )


def in_order(blocks, dim):
    blocks = jnp.moveaxis(blocks, 0, dim)
    dims = blocks.shape
    return blocks.reshape(*dims[:dim], dims[dim] * dims[dim + 1], *dims[dim + 2 :])


def gathered_copies(value, axis, dim):
    blocks = from_everyone(value, axis)
    return in_order(blocks, dim)


def stacked_from(value, axes, sequence):
    blocks = value[None]
    for k in sequence:
        blocks = lax.all_gather(blocks, axes[k], axis=0, tiled=True)
    block = [lax.axis_size(axes[k]) for k in reversed(sequence)]
    blocks = blocks.reshape(*block, *value.shape)
    turned = sorted(range(len(sequence)), key=lambda place: sequence[len(sequence) - 1 - place])
    return blocks.transpose(*turned, *range(len(sequence), blocks.ndim)).reshape(-1, *value.shape)


def gather_axes(value, axes, sequence, dim):
    return in_order(stacked_from(value, axes, sequence), dim)


def contract(left_rows, right_rows):
    return lax.dot_general(
        left_rows, right_rows, (((0,), (0,)), ((), ())), preferred_element_type=jnp.float32
    )


def local(window, weight, factor_a, factor_b, fitness):
    model_width = window.shape[1]
    cand_dev, factor_rank, _ = factor_a.shape
    shard_count = lax.axis_size(SHARD)
    total_cands = cand_dev * lax.axis_size("grp") * shard_count
    perturb = 0.25 / math.sqrt(model_width)
    step_scale = 0.5 / math.sqrt(total_cands)
    base_out = lax.dot_general(
        weight, window, (((1,), (1,)), ((), ())), preferred_element_type=jnp.float32
    )
    projected = jnp.einsum("td,crd->crt", window, factor_a, preferred_element_type=jnp.float32)
    projected_all, fitness_all = side_by_side((projected, fitness), SHARD, 0, 1)
    columns = lax.all_to_all(factor_b, SHARD, split_axis=2, concat_axis=0, tiled=True)
    col_width = columns.shape[2]
    low_rank = jnp.einsum(
        "crt,crf->fct", projected_all, columns.astype(jnp.float32), precision=lax.Precision.HIGHEST
    )
    perturbed = (
        (base_out[:, None, :] + perturb * low_rank).astype(jnp.bfloat16).reshape(col_width, -1)
    )
    weighted = (fitness_all[:, None, None] * columns.astype(jnp.float32)).astype(jnp.bfloat16)
    exchanged = lax.all_to_all(factor_a, "grp", split_axis=2, concat_axis=0, tiled=True)
    weighted_four = weighted.reshape(shard_count, cand_dev, factor_rank, col_width)
    weighted_flat = gathered_copies(weighted_four, "grp", 1).reshape(-1, col_width)
    owned_width = exchanged.shape[2]
    block_width = owned_width // 4
    update_parts = []
    for part_index in range(4):
        factor_slab = exchanged[:, :, part_index * block_width : (part_index + 1) * block_width]
        gathered = gather_axes(factor_slab, SHARD, (1, 0, 2), 0)
        update_parts.append(contract(weighted_flat, gathered.reshape(-1, block_width)))
    update = jnp.concatenate(update_parts, 1) * step_scale
    return (perturbed, update)


def solution(mesh):
    split = Mesh(
        mesh.devices.reshape(mesh.shape["grp"], 16, 2, 2), ("grp", "shard_0", "shard_1", "shard_2")
    )
    return jax.shard_map(
        local,
        mesh=split,
        in_specs=(
            P("grp", None),
            P(SHARD, None),
            P(GRP_SHARD, None, None),
            P(GRP_SHARD, None, None),
            P(GRP_SHARD),
        ),
        out_specs=(P(SHARD, "grp"), P(SHARD, "grp")),
        check_vma=False,
    )
```

profile of v0, /device:TPU:1, one launch (start us, length us, event | category | flops | bytes accessed | tf_op | source)
XLA Modules:
  0.0 370.5 jit_solution(10360211323301085646)
XLA Ops:
  7.2 4.5 %copy.56 = bf16[2,4,4096]{1,0,2:T(2,128)(2,1)S(1)} copy(bf16[2,4,4096]{2,1,0:T(4,128)(2,1)} %param.7) | data formatting | bytes 131072 | tf_op args[2]
  11.7 4.6 %reshape.55 = bf16[8,2,2048]{2,1,0:T(2,128)(2,1)} reshape(bf16[4096,2,4]{2,1,0:T(2,128)(2,1)S(1)} %bitcast.65) | data formatting | bytes 131072
  16.3 11.1 %all_to_all.41 = bf16[8,2,2048]{2,1,0:T(2,128)(2,1)} all-to-all(bf16[8,2,2048]{2,1,0:T(2,128)(2,1)} %reshape.55), channel_id=1, replica_groups=mesh['grp'=8,'shard_0'=16,'shard_1'=2,'shard_2'=2] {'grp'}, dimensions={0} | all-to-all | bytes 131072 | tf_op jit(solution)/shard_map/all_to_all | solution.py:83
  27.4 5.3 %reshape.56 = bf16[4096,2,4]{2,1,0:T(2,128)(2,1)S(1)} reshape(bf16[8,2,2048]{2,1,0:T(2,128)(2,1)} %all_to_all.41) | data formatting | bytes 131072
  32.7 3.3 copy.57
  36.8 4.8 %all-gather = bf16[32,4,128]{2,1,0:T(4,128)(2,1)S(1)} all-gather(bf16[16,4,128]{2,1,0:T(4,128)(2,1)S(1)} %get-tuple-element.12), channel_id=2, replica_groups=mesh['grp'=8,'shard_0'=16,'shard_1'=2,'shard_2'=2] {'shard_1'}, dimensions={0}, use_global_device_ids=true | all-gather | bytes 49152 | tf_op jit(solution)/shard_map/all_gather | solution.py:45
  41.6 34.3 %all_gather.41 = bf16[32,16,4,128]{3,1,2,0:T(8,128)(2,1)} all-gather(bf16[2,16,4,128]{3,1,2,0:T(8,128)(2,1)S(1)} %copy.58), channel_id=1, replica_groups=mesh['grp'=8,'shard_0'=16,'shard_1'=2,'shard_2'=2] {'shard_0'}, dimensions={0}, use_global_device_ids=true | all-gather | bytes 557056 | tf_op jit(solution)/shard_map/all_gather | solution.py:45
  76.0 4.8 %all-gather.1 = bf16[32,4,128]{2,1,0:T(4,128)(2,1)S(1)} all-gather(bf16[16,4,128]{2,1,0:T(4,128)(2,1)S(1)} %get-tuple-element.15), channel_id=3, replica_groups=mesh['grp'=8,'shard_0'=16,'shard_1'=2,'shard_2'=2] {'shard_1'}, dimensions={0}, use_global_device_ids=true | all-gather | bytes 49152 | tf_op jit(solution)/shard_map/all_gather | solution.py:45
  80.7 24.5 %all_gather.44 = bf16[32,16,4,128]{3,1,2,0:T(8,128)(2,1)} all-gather(bf16[2,16,4,128]{3,1,2,0:T(8,128)(2,1)S(1)} %copy.60), channel_id=1, replica_groups=mesh['grp'=8,'shard_0'=16,'shard_1'=2,'shard_2'=2] {'shard_0'}, dimensions={0}, use_global_device_ids=true | all-gather | bytes 557056 | tf_op jit(solution)/shard_map/all_gather | solution.py:45
  105.3 9.1 %copy.52 = bf16[2,4,11008]{1,0,2:T(2,128)(2,1)} copy(bf16[2,4,11008]{2,1,0:T(4,128)(2,1)S(1)} %copy-done.6) | data formatting | bytes 352256 | tf_op args[3]
  114.4 11.3 %reshape.53 = bf16[64,2,688]{2,1,0:T(2,128)(2,1)} reshape(bf16[11008,2,4]{2,1,0:T(2,128)(2,1)} %bitcast.62) | data formatting | bytes 352256
  125.6 28.1 %all-to-all-start = ((bf16[64,2,688]{2,1,0:T(2,128)(2,1)}), bf16[64,2,688]{2,1,0:T(2,128)(2,1)S(1)}, u32[]{:S(2)}, u32[]{:S(2)}) async-start(bf16[64,2,688]{2,1,0:T(2,128)(2,1)} %reshape.53), calls=%async_computation | async-start | bytes 393216 | tf_op jit(solution)/shard_map/all_to_all | solution.py:74
  153.9 5.1 %all-gather.2 = bf16[32,4,128]{2,1,0:T(4,128)(2,1)S(1)} all-gather(bf16[16,4,128]{2,1,0:T(4,128)(2,1)S(1)} %get-tuple-element.14), channel_id=4, replica_groups=mesh['grp'=8,'shard_0'=16,'shard_1'=2,'shard_2'=2] {'shard_1'}, dimensions={0}, use_global_device_ids=true | all-gather | bytes 49152 | tf_op jit(solution)/shard_map/all_gather | solution.py:45
  158.9 29.3 %all_gather.47 = bf16[32,16,4,128]{3,1,2,0:T(8,128)(2,1)} all-gather(bf16[2,16,4,128]{3,1,2,0:T(8,128)(2,1)S(1)} %copy.62), channel_id=1, replica_groups=mesh['grp'=8,'shard_0'=16,'shard_1'=2,'shard_2'=2] {'shard_0'}, dimensions={0}, use_global_device_ids=true | all-gather | bytes 557056 | tf_op jit(solution)/shard_map/all_gather | solution.py:45
  188.8 82.2 %all-gather.4 = f32[64,2,65]{2,1,0:T(2,128)S(1)} all-gather(f32[1,2,65]{2,1,0:T(2,128)S(1)} %maximum_bitcast_fusion), channel_id=1, replica_groups=mesh['grp'=8,'shard_0'=16,'shard_1'=2,'shard_2'=2] {'shard_0','shard_1',..., dimensions={0}, use_global_device_ids=true | all-gather | bytes 33800 | tf_op jit(solution)/shard_map/all_gather | solution.py:16
  271.9 4.8 %all-gather.3 = bf16[32,4,128]{2,1,0:T(4,128)(2,1)S(1)} all-gather(bf16[16,4,128]{2,1,0:T(4,128)(2,1)S(1)} %get-tuple-element.13), channel_id=5, replica_groups=mesh['grp'=8,'shard_0'=16,'shard_1'=2,'shard_2'=2] {'shard_1'}, dimensions={0}, use_global_device_ids=true | all-gather | bytes 49152 | tf_op jit(solution)/shard_map/all_gather | solution.py:45
  277.3 6.3 %reshape.54 = bf16[11008,2,4]{2,1,0:T(2,128)(2,1)} reshape(bf16[64,2,688]{2,1,0:T(2,128)(2,1)S(1)} %all-to-all-done) | data formatting | bytes 352256
  283.5 10.4 %copy.53 = bf16[2,4,64,172]{3,1,0,2:T(4,128)(2,1)S(1)} copy(bf16[2,4,64,172]{1,0,3,2:T(2,128)(2,1)} %bitcast.61) | data formatting | bytes 352256 | tf_op jit(solution)/shard_map/all_to_all | solution.py:74
  296.0 3.6 all-to-all-start.1
  299.7 26.3 %all_gather.50 = bf16[32,16,4,128]{3,1,2,0:T(8,128)(2,1)} all-gather(bf16[2,16,4,128]{3,1,2,0:T(8,128)(2,1)} %copy.64), channel_id=1, replica_groups=mesh['grp'=8,'shard_0'=16,'shard_1'=2,'shard_2'=2] {'shard_0'}, dimensions={0}, use_global_device_ids=true | all-gather | bytes 557056 | tf_op jit(solution)/shard_map/all_gather | solution.py:45
  330.5 3.1 fusion
  341.4 2.8 copy.63
  344.2 5.7 %all-gather.16.cloned.1.call-done = bf16[64,16,4,128]{3,1,2,0:T(8,128)(2,1)} async-done(((bf16[32,16,4,128]{3,1,2,0:T(8,128)(2,1)}), bf16[64,16,4,128]{3,1,2,0:T(8,128)(2,1)}) %all-gather.16.cloned.1.call-update) | async-done | bytes 1048592 | tf_op jit(solution)/shard_map/all_gather | solution.py:45
  355.2 3.1 reshape_reshape.3
  (59 shorter events, 28.3 us)
Async XLA Ops:
  7.2 322.0 %copy-start = (bf16[172,4096]{1,0:T(8,128)(2,1)S(1)}, bf16[172,4096]{1,0:T(8,128)(2,1)}, u32[]{:S(2)}) copy-start(bf16[172,4096]{1,0:T(8,128)(2,1)} %param.6) | copy-start | bytes 4227076
  7.2 328.7 %all-gather.10.cloned.1.call-start = ((), (), s32[]{:S(2)}) async-start(), calls=%async_computation.3 | async-start | bytes 1572864 | tf_op jit(solution)/shard_map/all_gather | solution.py:45
  36.0 69.3 %copy-start.6 = (bf16[2,4,11008]{2,1,0:T(4,128)(2,1)S(1)}, bf16[2,4,11008]{2,1,0:T(4,128)(2,1)}, u32[]{:S(2)}) copy-start(bf16[2,4,11008]{2,1,0:T(4,128)(2,1)} %param.8) | copy-start | bytes 528388
  75.9 262.7 %all-gather.12.cloned.1.call-start = ((), (), s32[]{:S(2)}) async-start(), calls=%async_computation.4 | async-start | bytes 1572864 | tf_op jit(solution)/shard_map/all_gather | solution.py:45
  114.4 73.9 %copy-start.7 = (bf16[16,4096]{1,0:T(8,128)(2,1)S(1)}, bf16[16,4096]{1,0:T(8,128)(2,1)}, u32[]{:S(2)}) copy-start(bf16[16,4096]{1,0:T(8,128)(2,1)} %param.5) | copy-start | bytes 393220
  114.4 73.9 %copy-start.8 = (bf16[2,4,4096]{2,1,0:T(4,128)(2,1)S(1)}, bf16[2,4,4096]{2,1,0:T(4,128)(2,1)}, u32[]{:S(2)}) copy-start(bf16[2,4,4096]{2,1,0:T(4,128)(2,1)} %param.7) | copy-start | bytes 196612
  114.4 74.2 %copy-start.9 = (f32[2]{0:T(128)S(1)}, f32[2]{0:T(128)}, u32[]{:S(2)}) copy-start(f32[2]{0:T(128)} %param.9) | copy-start | bytes 28
  125.6 151.6 %all-to-all-start = ((bf16[64,2,688]{2,1,0:T(2,128)(2,1)}), bf16[64,2,688]{2,1,0:T(2,128)(2,1)S(1)}, u32[]{:S(2)}, u32[]{:S(2)}) async-start(bf16[64,2,688]{2,1,0:T(2,128)(2,1)} %reshape.53), calls=%async_computation | async-start | bytes 393216 | tf_op jit(solution)/shard_map/all_to_all | solution.py:74
  153.8 187.6 %all-gather.14.cloned.1.call-start = ((), (), s32[]{:S(2)}) async-start(), calls=%async_computation.5 | async-start | bytes 1572864 | tf_op jit(solution)/shard_map/all_gather | solution.py:45
  271.0 0.6 copy-start.5
  293.9 2.1 copy-start.4
  296.0 56.7 %all-to-all-start.1 = ((bf16[8,64,2,4,172]{4,3,2,1,0:T(4,128)(2,1)}), bf16[8,64,2,4,172]{4,3,2,1,0:T(4,128)(2,1)S(1)}, u32[]{:S(2)}, u32[]{:S(2)}) async-start(bf16[8,64,2,4,172]{4,3,2,1,0:T(4,128)(2,1)} %broadcast_in_dim.18), calls=%async_computation.1 | async-start | bytes 4194304 | tf_op jit(solution)/shard_map/all_to_all | solution.py:26
  299.6 50.3 %all-gather.16.cloned.1.call-start = ((), (), s32[]{:S(2)}) async-start(), calls=%async_computation.6 | async-start | bytes 1572864 | tf_op jit(solution)/shard_map/all_gather | solution.py:45
  358.3 2.1 copy-start.1
  360.4 1.2 copy-start.2
  361.2 1.3 copy-start.3
Sparse Core Ops, SparseCore 0:
  76.0 23.9 all-gather.9
  105.4 32.8 all-gather.11
  188.4 23.9 all-gather.13
  326.1 23.6 all-gather.15
where the time goes:
time: 372 us; the launch traced here: 371 us
  blocking collectives  227 us (61%)
  local copies, waits for them, and re-layouts  81.6 us (22%)
  starting transfers between devices  31.9 us (9%)
  between operations  14 us (4%)
  matrix products  9.05 us (2%)
  waiting for transfers between devices  5.81 us (2%)
    all_gather x8, blocking collectives, stacked_from(): blocks = lax.all_gather(blocks, axes[k], axis=0, tiled=True)  134 us
    all_gather x1, blocking collectives, side_by_side(): filled, at, done = (lax.all_gather(both, axis, axis=dim, tiled=True), 0, [])  82.2 us
    unnamed x27, local copies, waits for them, and re-layouts  44.3 us
    all_to_all x1, starting transfers between devices, local(): lax.all_to_all(factor_b, SHARD, split_axis=2, concat_axis=0, tiled=True)  28.1 us
    all_to_all x1, blocking collectives, local(): lax.all_to_all(factor_a, 'grp', split_axis=2, concat_axis=0, tiled=True)  11.1 us
    transpose x4, local copies, waits for them, and re-layouts, stacked_from(): blocks.transpose(*turned, *range(len(sequence), blocks.ndim))  11.1 us
    all_to_all x1, local copies, waits for them, and re-layouts, local(): lax.all_to_all(factor_b, SHARD, split_axis=2, concat_axis=0, tiled=True)  10.4 us
  transfers between devices with their start and end apart: 6, of which 1 were waited for; matrix products, arithmetic and copies ran while one was open for 17% of the time, Pallas kernels for 0%

commit v1 on v0

v1 whole, which is shorter than its diff:
```python
import functools
import math

import jax
import jax.numpy as jnp
from jax import lax
from jax.experimental import pallas as pl
from jax.experimental.pallas import tpu as pltpu
from jax.sharding import Mesh
from jax.sharding import PartitionSpec as P

AXES = ("gy", "gx", "z", "yh", "core")
GRP = ("gy", "gx")
SHARD = ("z", "yh", "core")
MESH = pl.DeviceIdType.MESH
F32 = jnp.float32
BF16 = jnp.bfloat16
NZ, NG, NX = 16, 8, 4
ROWS = 8
WIDE = 768
OWN = 172
TAIL = OWN - 128
TAILPAD = 48


def remote(src, dst, ssem, rsem, **where):
    return pltpu.make_async_remote_copy(
        src_ref=src, dst_ref=dst, send_sem=ssem, recv_sem=rsem, device_id=where, device_id_type=MESH
    )


def dot_tn(left, right):
    return lax.dot_general(left, right, (((0,), (0,)), ((), ())), preferred_element_type=F32)


def dot_nt(left, right):
    return lax.dot_general(left, right, (((1,), (1,)), ((), ())), preferred_element_type=F32)


def columns_at(b_ref, start, at):
    width = b_ref.shape[1]
    base = min(start // 128 * 128, width - 256)
    pair = b_ref[:, base : base + 256].astype(F32)
    turn = (at - (start - base)) % 256
    if turn:
        pair = pltpu.roll(pair, turn, 1)
    return pair[:, :128]


def kernel(
    perturb, step_scale,
    fit_ref, win_ref, a_ref, b_ref, w_ref,
    pert_ref, upd_ref,
    wrep, bsend, ball, aall, bpert, wmat, amat, ubuf, basebuf, rs1, rs2s, rs2r,
    a1s, a1r, b1s, b1r, rgs, rgr, gxs, gxr, pxs, pxr, r1s, r1r, r2s, r2r,
):
    gy, gx, z, yh, core = (lax.axis_index(name) for name in AXES)
    g = gy * NX + gx
    ogy, oyh, ocore = 1 - gy, 1 - yh, 1 - core
    right, left = lax.rem(z + 1, NZ), lax.rem(z + NZ - 1, NZ)
    xr, xl, xo = lax.rem(gx + 1, NX), lax.rem(gx + 3, NX), lax.rem(gx + 2, NX)

    barrier = pltpu.get_barrier_semaphore()

    def greet(**where):
        pl.semaphore_signal(barrier, inc=1, device_id=where, device_id_type=MESH)

    for o in range(1, NZ):
        greet(z=lax.rem(z + o, NZ))
    for o in range(1, NG):
        p = lax.rem(g + o, NG)
        greet(gy=p // NX, gx=lax.rem(p, NX))
    greet(core=ocore)
    greet(yh=oyh)
    greet(yh=oyh, core=ocore)

    for k in range(8):
        wrep[16 * k : 16 * k + 16, :] = win_ref[...]
    proj = dot_nt(a_ref[...], wrep[...])
    high = proj.astype(BF16).astype(F32)
    low = proj - high
    lane = lax.broadcasted_iota(jnp.int32, (ROWS, 128), 1)
    row = lax.broadcasted_iota(jnp.int32, (ROWS, 128), 0)
    fit = jnp.where(row < ROWS // 2, fit_ref[0], fit_ref[1])
    fit0 = fit.astype(BF16).astype(F32)
    rest = fit - fit0
    fit1 = rest.astype(BF16).astype(F32)
    fit2 = rest - fit1
    extra = jnp.where(
        lane >= 112,
        low,
        jnp.where(lane >= 48, high, jnp.where(lane == 44, fit0, jnp.where(lane == 45, fit1, fit2))),
    )
    for k in range(NZ):
        first = 4 * OWN * k
        for j in range(4):
            bsend[k, :, 128 * j : 128 * j + 128] = columns_at(b_ref, first + OWN * j, 0).astype(BF16)
        for half in range(2):
            lo = columns_at(b_ref, first + OWN * (2 * half) + 128, 0)
            hi = columns_at(b_ref, first + OWN * (2 * half + 1) + 128, 64)
            tile = jnp.where(lane < TAIL, lo, jnp.where((lane >= 64) & (lane < 64 + TAIL), hi, extra))
            bsend[k, :, 512 + 128 * half : 640 + 128 * half] = tile.astype(BF16)
    mine = pl.ds(pl.multiple_of(g * 512, 512), 512)
    aall[z, g] = a_ref[:, mine]
    ball[gy, gx, z] = bsend[z]

    pl.semaphore_wait(barrier, NZ - 1 + NG - 1 + 3)

    a1 = []
    for o in range(1, NG):
        p = lax.rem(g + o, NG)
        cols = pl.ds(pl.multiple_of(p * 512, 512), 512)
        a1.append(
            remote(a_ref.at[:, cols], aall.at[z, g], a1s.at[o], a1r.at[o], gy=p // NX, gx=lax.rem(p, NX))
        )
        a1[-1].start()
    b1 = []
    for o in (8, 7, 9, 6, 10, 5, 11, 4, 12, 3, 13, 2, 14, 1, 15):
        p = lax.rem(z + o, NZ)
        b1.append(remote(bsend.at[p], ball.at[gy, gx, z], b1s.at[o], b1r.at[o], z=p))
        b1[-1].start()

    def a1_wait(o):
        p = lax.rem(g + NG - o, NG)
        remote(aall.at[z, p], aall.at[z, p], a1s.at[o], a1r.at[o], core=ocore).wait_recv()

    for o in range(1, NG):
        a1_wait(o)

    def ring(way, step, half):
        src = lax.rem(z + NZ - (step - 1), NZ) if way == 0 else lax.rem(z + step - 1, NZ)
        part = aall.at[src, pl.ds(4 * half, 4)]
        k = (way, step - 1, half)
        return remote(part, part, rgs.at[k], rgr.at[k], z=right if way == 0 else left)

    def ring_recv(way, step, half):
        src = lax.rem(z + NZ - step, NZ) if way == 0 else lax.rem(z + step, NZ)
        part = aall.at[src, pl.ds(4 * half, 4)]
        k = (way, step - 1, half)
        remote(part, part, rgs.at[k], rgr.at[k], z=right if way == 0 else left).wait_recv()

    def ring_has(way, step, half):
        return step < 8 or way == half

    def ring_go(step):
        for half in range(2):
            for way in range(2):
                if step > 1:
                    ring_recv(way, step - 1, half)
                if step < 9 and ring_has(way, step, half):
                    ring(way, step, half).start()

    ring_go(1)

    basebuf[...] = dot_nt(w_ref[...], wrep[...])

    ring_go(2)
    ring_go(3)

    for o in (1, 15, 2, 14, 3, 13, 4, 12, 5, 11, 6, 10, 7, 9, 8):
        p = lax.rem(z + NZ - o, NZ)
        remote(ball.at[gy, gx, p], ball.at[gy, gx, p], b1s.at[o], b1r.at[o], core=ocore).wait_recv()

    def gather(k, sy, sx, half, dest):
        part = ball.at[sy, sx, pl.ds(8 * half, 8)]
        return remote(part, part, gxs.at[k], gxr.at[k], **dest)

    sends = []

    def send(k, sy, sx, half, **dest):
        cp = gather(k, sy, sx, half, dest)
        cp.start()
        sends.append(cp)

    def got(k, sy, sx, half):
        gather(k, sy, sx, half, {"core": ocore}).wait_recv()

    for half in range(2):
        send(half, gy, gx, half, gy=ogy)
    for half in range(2):
        send(2 + half, gy, gx, half, gx=xr)
        send(4 + half, gy, gx, half, gx=xl)

    me = yh * 2 + core
    px = []
    for o, (py, pc) in enumerate(((yh, ocore), (oyh, core), (oyh, ocore))):
        main = pl.ds(pl.multiple_of((py * 2 + pc) * 128, 128), 128)
        tail = pl.ds(pl.multiple_of(512 + py * 128, 128), 128)
        for t, (lanes, at) in enumerate(((main, 0), (tail, 128))):
            px.append(
                remote(
                    ball.at[gy, gx, :, :, lanes], bpert.at[:, me, :, pl.ds(at, 128)],
                    pxs.at[o, t], pxr.at[o, t], yh=py, core=pc,
                )
            )
            px[-1].start()
    bpert[:, me, :, 0:128] = ball[gy, gx, :, :, pl.ds(pl.multiple_of(me * 128, 128), 128)]
    bpert[:, me, :, 128:256] = ball[gy, gx, :, :, pl.ds(pl.multiple_of(512 + yh * 128, 128), 128)]

    ring_go(4)
    ring_go(5)
    for half in range(2):
        got(half, ogy, gx, half)
    for half in range(2):
        send(6 + half, ogy, gx, half, gx=xr)
        send(8 + half, ogy, gx, half, gx=xl)
    got(2, gy, xl, 0)
    send(10, gy, xl, 0, gx=xr)
    got(5, gy, xr, 1)
    send(11, gy, xr, 1, gx=xl)
    ring_go(6)
    got(6, ogy, xl, 0)
    send(12, ogy, xl, 0, gx=xr)
    got(9, ogy, xr, 1)
    send(13, ogy, xr, 1, gx=xl)
    ring_go(7)

    for o, (py, pc) in enumerate(((yh, ocore), (oyh, core), (oyh, ocore))):
        for t in range(2):
            part = bpert.at[:, py * 2 + pc, :, pl.ds(128 * t, 128)]
            remote(part, part, pxs.at[o, t], pxr.at[o, t], core=ocore).wait_recv()
    lane_in = lax.broadcasted_iota(jnp.int32, (128, 128), 0)
    lane_out = lax.broadcasted_iota(jnp.int32, (128, 128), 1)
    pick_hi = (lane_in == 48 + lane_out % 16).astype(F32).astype(BF16)
    pick_lo = (lane_in == 112 + lane_out % 16).astype(F32).astype(BF16)
    pick_fit = ((lane_in >= 44) & (lane_in < 47)).astype(F32).astype(BF16)
    crow = lax.broadcasted_iota(jnp.int32, (128, 512), 0) // 4
    ccol = lax.broadcasted_iota(jnp.int32, (128, 512), 1) // 16
    same = crow == ccol

    def perturb_block(k, _):
        packets = bpert[pl.ds(4 * k, 4)].astype(F32).reshape(128, 256).astype(BF16)
        tail = packets[:, 128:]
        hi = jnp.dot(tail, pick_hi, preferred_element_type=F32)
        lo = jnp.dot(tail, pick_lo, preferred_element_type=F32)
        hi = jnp.where(same, jnp.concatenate([hi] * 4, axis=1), 0.0).astype(BF16)
        lo = jnp.where(same, jnp.concatenate([lo] * 4, axis=1), 0.0).astype(BF16)
        acc = dot_tn(packets, hi) + dot_tn(packets, lo)
        base = jnp.concatenate([basebuf[...]] * 4, axis=1)
        cols = pl.ds(pl.multiple_of(k * 512, 512), 512)
        pert_ref[0:128, cols] = (base[0:128] + perturb * acc[0:128]).astype(BF16)
        rem = jnp.where(core == 0, acc[128 : 128 + TAILPAD], acc[192 : 192 + TAILPAD])
        pert_ref[128:OWN, cols] = (base[128:OWN] + perturb * rem[:TAIL]).astype(BF16)
        return 0

    lax.fori_loop(0, 4, perturb_block, 0)

    ring_go(8)
    for k, sy, sx, half in (
        (3, gy, xl, 1), (4, gy, xr, 0), (7, ogy, xl, 1), (8, ogy, xr, 0),
        (10, gy, xo, 0), (11, gy, xo, 1), (12, ogy, xo, 0), (13, ogy, xo, 1),
    ):
        got(k, sy, sx, half)

    def weigh(p, _):
        packets = ball[p // NX, lax.rem(p, NX)].astype(F32).reshape(128, WIDE)
        fits = jnp.dot(packets[:, 512:640].astype(BF16), pick_fit, preferred_element_type=F32)
        fits = jnp.concatenate([fits] * 6, axis=1)
        wmat[pl.ds(pl.multiple_of(p * 128, 128), 128), :] = (packets * fits).astype(BF16)
        return 0

    lax.fori_loop(0, NG, weigh, 0)

    for way in range(2):
        ring_recv(way, 8, way)

    def flatten(p, _):
        rows = aall[:, p].astype(F32).reshape(128, 512)
        amat[pl.ds(pl.multiple_of(p * 128, 128), 128), :] = rows.astype(BF16)
        return 0

    lax.fori_loop(0, NG, flatten, 0)

    def product(k, _):
        rows = pl.ds(pl.multiple_of(k * 128, 128), 128)
        ubuf[rows, :] = dot_tn(wmat[:, rows], amat[...])
        return 0

    lax.fori_loop(0, 6, product, 0)

    def main_rows(py, pc):
        return pl.ds(pl.multiple_of((py * 2 + pc) * 128, 128), 128)

    def tail_rows(py, pc):
        return pl.ds(pl.multiple_of(512 + (py * 2 + pc) * 64, 64), TAILPAD)

    first = []
    for k, py in enumerate((oyh, yh)):
        first.append(
            remote(ubuf.at[main_rows(py, ocore)], rs1.at[k, pl.ds(0, 128)], r1s.at[k, 0], r1r.at[k, 0], core=ocore)
        )
        first.append(
            remote(ubuf.at[tail_rows(py, ocore)], rs1.at[k, pl.ds(128, TAILPAD)], r1s.at[k, 1], r1r.at[k, 1], core=ocore)
        )
    for cp in first:
        cp.start()
    first[0].wait_recv()
    first[1].wait_recv()
    rs2s[0:128, :] = ubuf[main_rows(oyh, core), :] + rs1[0, 0:128, :]
    rs2s[128:176, :] = ubuf[tail_rows(oyh, core), :] + rs1[0, 128:176, :]
    second = remote(rs2s, rs2r, r2s, r2r, yh=oyh)
    second.start()
    first[2].wait_recv()
    first[3].wait_recv()
    rs1[1, 0:128, :] = ubuf[main_rows(yh, core), :] + rs1[1, 0:128, :]
    rs1[1, 128:176, :] = ubuf[tail_rows(yh, core), :] + rs1[1, 128:176, :]
    second.wait_recv()
    upd_ref[...] = (rs1[1, 0:OWN, :] + rs2r[0:OWN, :]) * step_scale

    for cp in a1 + b1 + sends + px + first + [second]:
        cp.wait_send()
    for step in range(1, 9):
        for half in range(2):
            for way in range(2):
                if ring_has(way, step, half):
                    ring(way, step, half).wait_send()


def local(window, weight, factor_a, factor_b, fitness):
    d_model = window.shape[1]
    total = factor_a.shape[0] * NZ * 4 * NG
    perturb = 0.25 / math.sqrt(d_model)
    step_scale = 0.5 / math.sqrt(total)
    a8 = factor_a.reshape(ROWS, d_model)
    b8 = factor_b.reshape(ROWS, factor_b.shape[2])
    vmem = pl.BlockSpec(memory_space=pltpu.VMEM)
    dma = pltpu.SemaphoreType.DMA
    return pl.pallas_call(
        functools.partial(kernel, perturb, step_scale),
        name="es_step",
        out_shape=(
            jax.ShapeDtypeStruct((OWN, NZ * 128), BF16),
            jax.ShapeDtypeStruct((OWN, 512), F32),
        ),
        in_specs=[pl.BlockSpec(memory_space=pltpu.SMEM)] + [vmem] * 4,
        out_specs=(vmem, vmem),
        scratch_shapes=[
            pltpu.VMEM((128, d_model), BF16),
            pltpu.VMEM((NZ, ROWS, WIDE), BF16),
            pltpu.VMEM((2, NX, NZ, ROWS, WIDE), BF16),
            pltpu.VMEM((NZ, NG, ROWS, 512), BF16),
            pltpu.VMEM((NZ, 4, ROWS, 256), BF16),
            pltpu.VMEM((1024, WIDE), BF16),
            pltpu.VMEM((1024, 512), BF16),
            pltpu.VMEM((WIDE, 512), F32),
            pltpu.VMEM((OWN, 128), F32),
            pltpu.VMEM((2, 128 + TAILPAD, 512), F32),
            pltpu.VMEM((128 + TAILPAD, 512), F32),
            pltpu.VMEM((128 + TAILPAD, 512), F32),
            dma((NG,)), dma((NG,)), dma((NZ,)), dma((NZ,)),
            dma((2, 8, 2)), dma((2, 8, 2)), dma((14,)), dma((14,)),
            dma((3, 2)), dma((3, 2)), dma((2, 2)), dma((2, 2)), dma, dma,
        ],
        compiler_params=pltpu.CompilerParams(
            collective_id=0, has_side_effects=True, vmem_limit_bytes=48 * 1024 * 1024
        ),
    )(fitness, window, a8, b8, weight)


def solution(mesh):
    split = Mesh(mesh.devices.reshape(2, NX, NZ, 2, 2), AXES)
    return jax.shard_map(
        local,
        mesh=split,
        in_specs=(P(GRP, None), P(SHARD, None), P(GRP + SHARD, None, None), P(GRP + SHARD, None, None), P(GRP + SHARD)),
        out_specs=(P(SHARD, GRP), P(SHARD, GRP)),
        check_vma=False,
    )
```

time: 372 us -> 73.8 us (0.20)
  blocking collectives: 227 us -> 0 us
  local copies, waits for them, and re-layouts: 81.6 us -> 6.34 us
  Pallas kernels: 0 us -> 66.6 us
  starting transfers between devices: 31.9 us -> 0 us
  between operations: 14 us -> 0.65 us
  matrix products: 9.05 us -> 0 us
  waiting for transfers between devices: 5.81 us -> 0 us
    all_gather x9 -> x0, blocking collectives: 216 us -> none  [the longest x8 134 us: stacked_from(): blocks = lax.all_gather(blocks, axes[k], axis=0, tiled=True)]
    pallas_call x0 -> x1, Pallas kernels: none -> 66.6 us  [local(): pl.pallas_call(functools.partial(kernel, perturb, step_scale), name='es_s...]
    unnamed x27 -> x8, local copies, waits for them, and re-layouts: 44.3 us -> 4.51 us
    all_to_all x2 -> x0, starting transfers between devices: 31.7 us -> none  [the longest x1 28.1 us: local(): lax.all_to_all(factor_b, SHARD, split_axis=2, concat_axis=0, tiled=True)]
    all_to_all x2 -> x0, local copies, waits for them, and re-layouts: 13.7 us -> none  [the longest x1 10.4 us: local(): lax.all_to_all(factor_b, SHARD, split_axis=2, concat_axis=0, tiled=True)]
    transpose x5 -> x0, local copies, waits for them, and re-layouts: 13.6 us -> none  [the longest x4 11.1 us: stacked_from(): blocks.transpose(*turned, *range(len(sequence), blocks.ndim))]
    all_to_all x1 -> x0, blocking collectives: 11.1 us -> none  [local(): lax.all_to_all(factor_a, 'grp', split_axis=2, concat_axis=0, tiled=True)]
    dot_general x7 -> x0, matrix products: 9.05 us -> none  [the longest x4 4.33 us: contract(): lax.dot_general(left_rows, right_rows, (((0,), (0,)), ((), ())), preferre...]
  transfers between devices with their start and end apart: 6 -> 0, of which waited for: 1 -> 0; matrix products, arithmetic and copies ran while one was open for 17% -> 0% of each run, Pallas kernels for 0% -> 0%
where the time goes in v1:
time: 73.8 us; the launch traced here: 73.6 us
  Pallas kernels  66.6 us (90%)
  local copies, waits for them, and re-layouts  6.34 us (9%)
    pallas_call x1, Pallas kernels, local(): pl.pallas_call(functools.partial(kernel, perturb, step_scale), name='es_s...  66.6 us
    unnamed x8, local copies, waits for them, and re-layouts  4.51 us

profile of v1, /device:TPU:1, one launch (start us, length us, event | category | flops | bytes accessed | tf_op | source)
XLA Modules:
  0.0 73.6 jit_solution(8588183256901465323)
XLA Ops:
  0.6 0.9 %reshape.10.a_ref = bf16[8,4096]{1,0:T(8,128)(2,1)S(1)} reshape(bf16[2,4,4096]{2,1,0:T(4,128)(2,1)} %param.7) | data formatting | bytes 131072 | tf_op jit(solution)/shard_map/reshape | solution.py:324
  1.5 1.0 %reshape.11.b_ref = bf16[8,11008]{1,0:T(8,128)(2,1)S(1)} reshape(bf16[2,4,11008]{2,1,0:T(4,128)(2,1)} %param.8) | data formatting | bytes 352256 | tf_op jit(solution)/shard_map/reshape | solution.py:325
  2.5 0.0 copy-start
  2.5 1.4 %copy-done = bf16[172,4096]{1,0:T(8,128)(2,1)S(1)} copy-done((bf16[172,4096]{1,0:T(8,128)(2,1)S(1)}, bf16[172,4096]{1,0:T(8,128)(2,1)}, u32[]{:S(2)}) %copy-start) | copy-done | bytes 1409048
  3.8 0.0 copy-start.1
  3.8 0.9 %copy-done.1 = bf16[16,4096]{1,0:T(8,128)(2,1)S(1)} copy-done((bf16[16,4096]{1,0:T(8,128)(2,1)S(1)}, bf16[16,4096]{1,0:T(8,128)(2,1)}, u32[]{:S(2)}) %copy-start.1) | copy-done | bytes 131096
  4.7 0.0 copy-start.2
  4.7 0.7 copy-done.2
  5.4 66.6 %es_step.1 = (bf16[172,2048]{1,0:T(8,128)(2,1)S(1)}, f32[172,512]{1,0:T(8,128)S(1)}) custom-call(f32[2]{0:T(128)S(1)} %copy-done.2, bf16[16,4096]{1,0:T(8,128)(2,1)S(1)} %copy-done.1, bf16[8,4096]{1,0:T(8,128)(2,1)S(1)} %reshape.10.a_ref, bf16[8,11008]{1,0:T(8,128)(2,1)S(1)} %reshape.11.b_ref, bf16[172,4096]{1,0:T(8,128)(2,1)S(1)} %copy-done), custom_call_target="tpu_custom_call" | custom-call | tf_op jit(solution)/shard_map/es_step/pallas_call | solution.py:328
  72.0 0.9 %copy.9 = bf16[172,2048]{1,0:T(8,128)(2,1)} copy(bf16[172,2048]{1,0:T(8,128)(2,1)S(1)} %get-tuple-element.4) | data formatting | bytes 1409024
  72.9 0.7 copy.10
Async XLA Ops:
  2.5 1.4 %copy-start = (bf16[172,4096]{1,0:T(8,128)(2,1)S(1)}, bf16[172,4096]{1,0:T(8,128)(2,1)}, u32[]{:S(2)}) copy-start(bf16[172,4096]{1,0:T(8,128)(2,1)} %w_ref.1) | copy-start | bytes 4227076
  3.8 0.9 %copy-start.1 = (bf16[16,4096]{1,0:T(8,128)(2,1)S(1)}, bf16[16,4096]{1,0:T(8,128)(2,1)}, u32[]{:S(2)}) copy-start(bf16[16,4096]{1,0:T(8,128)(2,1)} %win_ref.1) | copy-start | bytes 393220
  4.7 0.7 copy-start.2
